TPU v7x, 16 devices: a whole 2x2x2 slice. The times are simulated.
16 devices in a mesh: graph: 16 (over z, y, x, core).
Axes of the slice: x: 2, y: 2, z: 2, core: 2. Of those that a mesh axis runs over, the one named last changes fastest.
Arguments:
- feats: bfloat16 [32768, 500], P('graph')
- w_one: float32 [500, 256], replicated
- w_two: float32 [256, 7], replicated
- send_idx: int32 [256, 64], P('graph')
- send_count: int32 [256], P('graph')
- edge_src: int32 [32768, 12], P('graph')
- edge_wt: float32 [32768, 12], P('graph')
- labels: int32 [32768], P('graph')
- label_mask: int32 [32768], P('graph')
Outputs:
- output 1: float32 [], replicated
- output 2: float32 [500, 256], replicated
- output 3: float32 [256, 7], replicated
All inputs are finite; a program needn't handle non-finite values.
Results may differ from a plain program's by a relative error of at most 0.001.
Values are sent between devices in bfloat16 or wider.
A program may use at most 1 GiB of HBM per device.

v0:
```python
import jax
import jax.numpy as jnp
from jax import lax
from jax.sharding import PartitionSpec as P


def solution(mesh):
    dev_count = mesh.shape["graph"]

    def device_step(feats, w_one, w_two, send_idx, send_count, edge_src, edge_wt, labels, label_mask):
        row_count = feats.shape[0]
        halo_rows = send_idx.shape[1]
        in_deg = edge_src.shape[1]
        list_ids = send_idx.reshape(dev_count * halo_rows)
        list_ok = (jnp.arange(halo_rows)[None, :] < send_count[:, None]).reshape(dev_count * halo_rows, 1)
        flat_src = edge_src.reshape(row_count * in_deg)
        w_one_b = w_one.astype(jnp.bfloat16)
        w_two_b = w_two.astype(jnp.bfloat16)

        def aggregate(h_rows):
            outgoing = jnp.where(list_ok, h_rows[list_ids], 0)
            incoming = lax.all_to_all(outgoing, "graph", 0, 0, tiled=True)
            ext_rows = jnp.concatenate([h_rows, incoming], axis=0)
            return jnp.sum(ext_rows[edge_src].astype(jnp.float32) * edge_wt[:, :, None], axis=1)

        z_one = aggregate(feats).astype(jnp.bfloat16)
        h_one = jnp.maximum(jnp.dot(z_one, w_one_b, preferred_element_type=jnp.float32), 0.0).astype(jnp.bfloat16)
        z_two = aggregate(h_one).astype(jnp.bfloat16)
        logits = jnp.dot(z_two, w_two_b, preferred_element_type=jnp.float32)
        mask_f = label_mask.astype(jnp.float32)
        label_total = lax.psum(jnp.sum(mask_f), "graph")
        log_prob = jax.nn.log_softmax(logits, axis=-1)
        onehot = (labels[:, None] == jnp.arange(logits.shape[1])[None, :]).astype(jnp.float32)
        loss_val = -lax.psum(jnp.sum(mask_f[:, None] * onehot * log_prob), "graph") / label_total
        d_logits = ((jnp.exp(log_prob) - onehot) * (mask_f / label_total)[:, None]).astype(jnp.bfloat16)
        grad_two = lax.psum(jnp.einsum("nf,nc->fc", z_two, d_logits, preferred_element_type=jnp.float32), "graph")
        d_z2 = jnp.einsum("nc,fc->nf", d_logits, w_two_b, preferred_element_type=jnp.float32)
        contrib = (edge_wt[:, :, None] * d_z2[:, None, :]).reshape(row_count * in_deg, d_z2.shape[1])
        ext_grad = jax.ops.segment_sum(contrib, flat_src, num_segments=row_count + dev_count * halo_rows)
        returned = lax.all_to_all(ext_grad[row_count:], "graph", 0, 0, tiled=True)
        d_h1 = ext_grad[:row_count] + jax.ops.segment_sum(jnp.where(list_ok, returned, 0.0), list_ids, num_segments=row_count)
        d_y1 = jnp.where(h_one > 0, d_h1, 0.0).astype(jnp.bfloat16)
        grad_one = lax.psum(jnp.einsum("nf,nh->fh", z_one, d_y1, preferred_element_type=jnp.float32), "graph")
        return loss_val, grad_one, grad_two

    row_spec = P("graph", None)
    vec_spec = P("graph")
    return jax.shard_map(device_step, mesh=mesh, in_specs=(row_spec, P(), P(), row_spec, vec_spec, row_spec, row_spec, vec_spec, vec_spec), out_specs=(P(), P(), P()), check_vma=False)
```

profile of v0, /device:TPU:0, one launch (start us, length us, event | category | flops | bytes accessed | tf_op | source)
XLA Modules:
  0.0 688.2 jit_solution(7353568814505531615)
XLA Ops:
  7.2 2.9 copy.17
  10.1 0.1 reshape.84
  10.2 0.1 iota_compare_fusion.1
  10.3 4.0 gather_fusion
  14.3 1.2 broadcast_select_fusion
  15.5 5.3 all-to-all-start
  20.8 0.4 copy.18
  21.2 0.9 reshape.95
  22.0 1.4 copy.19
  23.4 13.4 %all-to-all-done = bf16[16,64,500]{2,1,0:T(8,128)(2,1)S(1)} async-done(((bf16[16,64,500]{2,1,0:T(8,128)(2,1)}), bf16[16,64,500]{2,1,0:T(8,128)(2,1)S(1)}, u32[]{:S(2)}, u32[]{:S(2)}) %all-to-all-start) | async-done | bytes 1024032 | tf_op jit(solution)/shard_map/all_to_all | solution.py:22
  36.9 1.0 copy-done.7
  37.9 2.3 pad_maximum_fusion
  40.2 98.7 %gather_fusion.1 = bf16[24576,500]{1,0:T(8,128)(2,1)} fusion(bf16[3072,500]{1,0:T(8,128)(2,1)S(1)} %pad_maximum_fusion, s32[24576]{0:T(1024)S(1)} %broadcast_clamp_fusion), kind=kCustom, calls=%fused_computation.1 | custom fusion | bytes 49250304 | tf_op jit(solution)/shard_map/gather | solution.py:24
  138.9 45.8 %reshape.139 = f32[2048,12,500]{2,1,0:T(8,128)} reshape(bf16[24576,500]{1,0:T(8,128)(2,1)} %gather_fusion.1) | data formatting | bytes 73728000 | tf_op jit(solution)/shard_map/convert_element_type | solution.py:24
  184.8 23.1 %multiply_reduce_fusion = bf16[2048,500]{1,0:T(8,128)(2,1)} fusion(f32[2048,12,500]{2,1,0:T(8,128)} %reshape.139, f32[2048,12]{1,0:T(8,128)S(1)} %copy-done.4), kind=kLoop, calls=%fused_computation.6 | loop fusion | flops 23552000 | bytes 51298304 | tf_op jit(solution)/shard_map/reduce_sum | solution.py:24
  207.8 2.3 fusion.3
  210.2 3.9 gather_fusion.2
  214.1 1.0 broadcast_select_fusion.1
  215.1 2.3 all-to-all-start.1
  217.4 0.6 convert_reduce_fusion
  218.1 34.0 %psum.29 = f32[]{:T(128)} all-reduce(f32[]{:T(128)} %convert_reduce_fusion), channel_id=1, replica_groups=mesh['graph'=16] {'graph'}, use_global_device_ids=true, to_apply=%region_7.8 | all-reduce | flops 1 | bytes 8 | tf_op jit(solution)/shard_map/psum | solution.py:31
  252.0 0.8 mul.60
  252.9 0.4 copy.21
  253.2 0.9 reshape.119
  254.1 0.6 broadcast_divide_fusion
  254.7 0.1 pad_maximum_fusion.1
  254.9 96.7 %gather_fusion.3 = bf16[24576,256]{1,0:T(8,128)(2,1)} fusion(bf16[3072,256]{1,0:T(8,128)(2,1)S(1)} %pad_maximum_fusion.1, s32[24576]{0:T(1024)S(1)} %broadcast_clamp_fusion), kind=kCustom, calls=%fused_computation.3 | custom fusion | bytes 25264128 | tf_op jit(solution)/shard_map/gather | solution.py:24
  351.5 22.7 %reshape.140 = f32[2048,12,256]{2,1,0:T(8,128)} reshape(bf16[24576,256]{1,0:T(8,128)(2,1)} %gather_fusion.3) | data formatting | bytes 37748736 | tf_op jit(solution)/shard_map/convert_element_type | solution.py:24
  374.2 16.5 %multiply_reduce_fusion.1 = bf16[2048,256]{1,0:T(8,128)(2,1)S(1)} fusion(f32[2048,12,256]{2,1,0:T(8,128)} %reshape.140, f32[2048,12]{1,0:T(8,128)S(1)} %copy-done.5), kind=kLoop, calls=%fused_computation.7 | loop fusion | flops 12058624 | bytes 26312704 | tf_op jit(solution)/shard_map/reduce_sum | solution.py:24
  390.7 1.0 copy-done.6
  391.7 0.4 fusion.20
  392.2 0.5 fusion.15
  392.7 11.1 %mul.64 = f32[2048,12,256]{2,1,0:T(8,128)} broadcast(f32[2048,256]{1,0:T(8,128)S(1)} %fusion.15), dimensions={0,2} | broadcast | bytes 27262976 | tf_op jit(solution)/shard_map/mul | solution.py:38
  403.8 30.0 %mul.65 = f32[24576,256]{1,0:T(8,128)} reshape(f32[2048,12,256]{2,1,0:T(8,128)} %mul.64) | data formatting | bytes 50331648 | tf_op jit(solution)/shard_map/mul | solution.py:38
  433.8 145.1 %scatter_custom_fusion = f32[3072,256]{1,0:T(8,128)S(1)} fusion(s32[24576]{0:T(1024)S(1)} %reshape.119, f32[24576,256]{1,0:T(8,128)} %mul.65, f32[24576]{0:T(1024)S(1)} %mul.60, f32[]{:T(128)} %constant.6.clone.1), kind=kCustom, calls=%fused_computation.8 | custom fusion | flops 12582912 | bytes 28409860 | tf_op jit(solution)/shard_map/scatter-add | solution.py:39
  578.9 1.1 slice.17
  580.0 3.3 all-to-all-start.2
  583.4 0.1 lt.41
  583.5 0.1 reshape.127
  583.6 15.9 %all-to-all-done.2 = f32[16,64,256]{2,1,0:T(8,128)} async-done(((f32[16,64,256]{2,1,0:T(8,128)}), f32[16,64,256]{2,1,0:T(8,128)}, u32[]{:S(2)}, u32[]{:S(2)}) %all-to-all-start.2) | async-done | bytes 1048608 | tf_op jit(solution)/shard_map/all_to_all | solution.py:40
  599.5 2.5 bitcast_select_fusion
  602.0 7.3 %scatter_fusion = f32[2048,256]{1,0:T(8,128)S(1)} fusion(f32[2048,256]{1,0:T(8,128)S(1)} %slice-done, s32[1024]{0:T(1024)S(1)} %reshape.127, f32[1024,256]{1,0:T(8,128)} %bitcast_select_fusion), kind=kCustom, calls=%fused_computation.5 | custom fusion | flops 262144 | bytes 3149824 | tf_op jit(solution)/shard_map/scatter-add | solution.py:41
  609.3 3.1 fusion.5
  612.5 1.5 fusion.10
  614.0 0.6 multiply_reduce_fusion.2
  614.6 32.0 %all-reduce = (f32[]{:T(128)}, f32[256,7]{0,1:T(8,128)}) all-reduce(f32[]{:T(128)} %multiply_reduce_fusion.2, f32[256,7]{0,1:T(8,128)S(1)} %fusion.10), channel_id=1, replica_groups=mesh['graph'=16] {'graph'}, use_global_device_ids=true, to_apply=%region_5.6 | all-reduce | flops 1793 | bytes 14344 | tf_op jit(solution)/shard_map/psum | solution.py:34
  647.9 30.5 %all-reduce.3.cloned.1.call-done = f32[500,256]{1,0:T(8,128)} async-done(((f32[500,256]{1,0:T(8,128)}), f32[500,256]{1,0:T(8,128)}) %all-reduce.3.cloned.1.call-update) | async-done | bytes 512016 | tf_op jit(solution)/shard_map/psum | solution.py:43
  678.4 1.9 copy.25
  (44 shorter events, 0.2 us)
Async XLA Ops:
  7.2 2.9 copy-start.13
  7.2 3.0 copy-start.15
  10.1 4.2 copy-start
  14.2 6.5 copy-start.8
  14.3 7.8 %copy-start.9 = (f32[2048,12]{0,1:T(8,128)S(1)}, f32[2048,12]{0,1:T(8,128)}, u32[]{:S(2)}) copy-start(f32[2048,12]{0,1:T(8,128)} %param.15) | copy-start | bytes 294916
  15.5 21.4 %all-to-all-start = ((bf16[16,64,500]{2,1,0:T(8,128)(2,1)}), bf16[16,64,500]{2,1,0:T(8,128)(2,1)S(1)}, u32[]{:S(2)}, u32[]{:S(2)}) async-start(bf16[16,64,500]{2,1,0:T(8,128)(2,1)} %broadcast_select_fusion), calls=%async_computation | async-start | bytes 2097152 | tf_op jit(solution)/shard_map/all_to_all | solution.py:22
  36.9 1.0 copy-start.7
  138.9 45.8 %copy-start.4 = (f32[2048,12]{1,0:T(8,128)S(1)}, f32[2048,12]{1,0:T(8,128)}, u32[]{:S(2)}) copy-start(f32[2048,12]{1,0:T(8,128)} %copy.19) | copy-start | bytes 294916
  184.7 23.1 %copy-start.16 = (f32[500,256]{1,0:T(8,128)S(1)}, f32[500,256]{1,0:T(8,128)}, u32[]{:S(2)}) copy-start(f32[500,256]{1,0:T(8,128)} %param.10) | copy-start | bytes 1536004
  210.1 44.6 %copy-start.2 = (bf16[2048,256]{1,0:T(8,128)(2,1)}, bf16[2048,256]{1,0:T(8,128)(2,1)S(1)}, u32[]{:S(2)}) copy-start(bf16[2048,256]{1,0:T(8,128)(2,1)S(1)} %fusion.3) | copy-start | bytes 3145732
  210.1 7.3 %copy-start.11 = (s32[2048]{0:T(1024)S(1)}, s32[2048]{0:T(1024)}, u32[]{:S(2)}) copy-start(s32[2048]{0:T(1024)} %param.17) | copy-start | bytes 24580
  215.1 39.6 %all-to-all-start.1 = ((bf16[16,64,256]{2,1,0:T(8,128)(2,1)}), bf16[16,64,256]{2,1,0:T(8,128)(2,1)S(1)}, u32[]{:S(2)}, u32[]{:S(2)}) async-start(bf16[16,64,256]{2,1,0:T(8,128)(2,1)} %broadcast_select_fusion.1), calls=%async_computation.1 | async-start | bytes 1048576 | tf_op jit(solution)/shard_map/all_to_all | solution.py:22
  351.5 22.7 %copy-start.5 = (f32[2048,12]{1,0:T(8,128)S(1)}, f32[2048,12]{1,0:T(8,128)}, u32[]{:S(2)}) copy-start(f32[2048,12]{1,0:T(8,128)} %copy.19) | copy-start | bytes 294916
  374.2 17.5 %copy-start.12 = (f32[256,7]{0,1:T(8,128)S(1)}, f32[256,7]{0,1:T(8,128)}, u32[]{:S(2)}) copy-start(f32[256,7]{0,1:T(8,128)} %param.11) | copy-start | bytes 21508
  374.2 18.0 %copy-start.10 = (s32[2048]{0:T(1024)S(1)}, s32[2048]{0:T(1024)}, u32[]{:S(2)}) copy-start(s32[2048]{0:T(1024)} %param.16) | copy-start | bytes 24580
  390.7 1.0 copy-start.6
  578.9 4.7 copy-start.1
  578.9 4.6 copy-start.14
  580.0 19.4 %all-to-all-start.2 = ((f32[16,64,256]{2,1,0:T(8,128)}), f32[16,64,256]{2,1,0:T(8,128)}, u32[]{:S(2)}, u32[]{:S(2)}) async-start(f32[16,64,256]{2,1,0:T(8,128)} %bitcast.13), calls=%async_computation.2 | async-start | bytes 2097152 | tf_op jit(solution)/shard_map/all_to_all | solution.py:40
  583.4 95.0 %all-reduce.3.cloned.1.call-start = ((), (), s32[]{:S(2)}) async-start(), calls=%async_computation.3 | async-start | bytes 1032192 | tf_op jit(solution)/shard_map/psum | solution.py:43
  599.5 2.5 slice-start
  602.0 7.3 %copy-start.3 = (bf16[2048,256]{1,0:T(8,128)(2,1)S(1)}, bf16[2048,256]{1,0:T(8,128)(2,1)}, u32[]{:S(2)}) copy-start(bf16[2048,256]{1,0:T(8,128)(2,1)} %copy-done.2) | copy-start | bytes 3145732
Sparse Core Ops, SparseCore 0:
  612.6 65.6 all-reduce.2
where the time goes:
time: 692 us; the launch traced here: 688 us
  local copies, waits for them, and re-layouts  326 us (47%)
  other arithmetic  201 us (29%)
  blocking collectives  65.9 us (10%)
  waiting for transfers between devices  59.8 us (9%)
  between operations  16.8 us (2%)
  starting transfers between devices  11 us (2%)
  matrix products  7.77 us (1%)
    gather x2, local copies, waits for them, and re-layouts, aggregate(): ext_rows[edge_src].astype(jnp.float32) * edge_wt[:, :, None]  195 us
    scatter-add x1, other arithmetic, device_step(): jax.ops.segment_sum(contrib, flat_src, num_segments=row_count + dev_count...  145 us
    convert_element_type x2, local copies, waits for them, and re-layouts, aggregate(): ext_rows[edge_src].astype(jnp.float32) * edge_wt[:, :, None]  68.5 us
    mul x2, local copies, waits for them, and re-layouts, device_step(): edge_wt[:, :, None] * d_z2[:, None, :]  41.1 us
    reduce_sum x2, other arithmetic, aggregate(): jnp.sum(ext_rows[edge_src].astype(jnp.float32) * edge_wt[:, :, None], axi...  39.5 us
    psum x1, blocking collectives, device_step(): label_total = lax.psum(jnp.sum(mask_f), 'graph')  34 us
    psum x1, blocking collectives, device_step(): lax.psum(jnp.sum(mask_f[:, None] * onehot * log_prob), 'graph')  32 us
    psum x1, waiting for transfers between devices, device_step(): lax.psum(jnp.einsum('nf,nh->fh', z_one, d_y1, preferred_element_type=jnp....  30.5 us
  transfers between devices with their start and end apart: 4, of which 3 were waited for; matrix products, arithmetic and copies ran while one was open for 1% of the time, Pallas kernels for 0%

commit v1 on v0

v1 whole, which is shorter than its diff:
```python
import functools

import jax
import jax.numpy as jnp
from jax import lax
from jax.experimental import pallas as pl
from jax.experimental.pallas import tpu as pltpu
from jax.sharding import PartitionSpec as P

DEVS = 16
ROWS = 2048
HALO = 64
DEG = 12
FIN = 500
FPAD = 512
HID = 256
CLS = 7
EXT = ROWS + DEVS * HALO
BM = 256
NB = ROWS // BM
PIECES = 3
TILES = EXT // 128
F32 = jnp.float32
BF16 = jnp.bfloat16
BIG = 3.3895313892515355e38


def split3(x):
    hi = jnp.minimum(jnp.maximum(x, -BIG), BIG).astype(BF16)
    r = x - hi.astype(F32)
    mid = r.astype(BF16)
    lo = (r - mid.astype(F32)).astype(BF16)
    return hi, mid, lo


def code_of(i):
    return jnp.left_shift(128 + jnp.bitwise_and(i, 127), jnp.right_shift(i, 7))


def kernel(feats, w1, w2, sidx, scnt, esrc, ewt, labels, lmask,
           loss_o, g1_o, g2_o,
           a3, e1, z1, e2, z2, sel, send1, send2, srcp, wtp, codes, whi, wmid, wlo, iocode, lcode,
           w1b, w2s, cnts, cnt_own, sendu, recvu, small, smallr, rt, part, rsr, red, agb, ut,
           ssem, rsem):
    me = lax.axis_index("graph")

    def peer(d):
        return lax.rem(me + d, DEVS)

    bar = pltpu.get_barrier_semaphore()
    for d in range(1, DEVS):
        pl.semaphore_signal(bar, inc=1, device_id=(peer(d),), device_id_type=pl.DeviceIdType.MESH)

    def remote(phase, d, src, dst):
        return pltpu.make_async_remote_copy(
            src_ref=src, dst_ref=dst, send_sem=ssem.at[phase, d], recv_sem=rsem.at[phase, d],
            device_id=(peer(d),), device_id_type=pl.DeviceIdType.MESH)

    lane16 = lax.broadcasted_iota(jnp.int32, (16, 128), 1)
    for t in range(TILES):
        iocode[t] = code_of(lane16 + 128 * t).astype(F32).astype(BF16)

    lcode[...] = jnp.zeros(lcode.shape, jnp.int32)
    lcode[0:DEVS, 0:HALO] = sidx[...]
    idx_t = lcode[...].T
    pos = lax.broadcasted_iota(jnp.int32, (128, 128), 0)
    cnt_l = jnp.zeros((128, 128), jnp.int32)
    lcode[0:1, 0:DEVS] = scnt[...]
    cnt_row = lcode[0:1, :]
    ok = (pos < cnt_row) & (lax.broadcasted_iota(jnp.int32, (128, 128), 1) < DEVS)
    lc = jnp.where(ok, code_of(jnp.bitwise_and(idx_t, ROWS - 1)), 0).astype(F32).astype(BF16)
    for q in range(DEVS):
        col = jnp.broadcast_to(lc[0:HALO, q:q + 1], (HALO, 128))
        for t in range(ROWS // 128):
            io = jnp.concatenate([iocode[t]] * (HALO // 16), axis=0)
            sel[q * HALO:(q + 1) * HALO, t * 128:(t + 1) * 128] = jnp.where(
                col == io, jnp.ones((HALO, 128), BF16), jnp.zeros((HALO, 128), BF16))

    e1[0:ROWS, 384:512] = jnp.zeros((ROWS, 128), BF16)
    e1[0:ROWS, 0:FIN] = feats[...]
    own = pl.multiple_of(ROWS + me * HALO, HALO)
    e1[pl.ds(own, HALO), :] = jnp.zeros((HALO, FPAD), BF16)
    e2[pl.ds(own, HALO), :] = jnp.zeros((HALO, HID), BF16)
    for b in range(4):
        send1[b * 256:(b + 1) * 256, :] = jnp.dot(
            sel[b * 256:(b + 1) * 256, :], e1[0:ROWS, :], preferred_element_type=F32).astype(BF16)
    maskf = lmask[...].astype(F32)
    cnt_own[...] = jnp.broadcast_to(jnp.sum(maskf, axis=1, keepdims=True), (8, 128))
    cnts[me] = cnt_own[...]

    pl.semaphore_wait(bar, DEVS - 1)
    first = []
    for d in range(1, DEVS):
        src = pl.multiple_of(peer(d) * HALO, HALO)
        first.append(remote(0, d, send1.at[pl.ds(src, HALO), :], e1.at[pl.ds(own, HALO), :]))
        first.append(remote(1, d, cnt_own, cnts.at[me]))
    for c in first:
        c.start()

    w1b[...] = jnp.zeros(w1b.shape, BF16)
    w1b[0:FIN, :] = w1[...].astype(BF16)
    w2s[...] = jnp.zeros(w2s.shape, F32)
    w2s[:, 0:CLS] = w2[...]
    w2t = w2s[...].T[0:8, :].astype(BF16)

    def prep(i, carry):
        r = pl.multiple_of(i * 128, 128)
        srcp[...] = jnp.full(srcp.shape, -1, jnp.int32)
        wtp[...] = jnp.zeros(wtp.shape, F32)
        srcp[:, 0:DEG] = esrc[pl.ds(r, 128), :]
        wtp[:, 0:DEG] = ewt[pl.ds(r, 128), :]
        s = srcp[...]
        w = wtp[...]
        tot = w
        for j in range(1, DEG):
            tot = tot + jnp.where(pltpu.roll(s, j, 1) == s, pltpu.roll(w, j, 1), 0.0)
        hi, mid, lo = split3(tot)
        whi[pl.ds(r, 128), :] = hi
        wmid[pl.ds(r, 128), :] = mid
        wlo[pl.ds(r, 128), :] = lo
        codes[pl.ds(r, 128), :] = jnp.where(s < 0, 0, code_of(jnp.maximum(s, 0))).astype(F32).astype(BF16)
        return carry

    lax.fori_loop(0, ROWS // 128, prep, 0)

    def build(g, carry):
        r = pl.multiple_of(g * 16, 16)
        base = pl.multiple_of((g // 16) * (BM * PIECES) + lax.rem(g, 16) * 16, 16)
        cg, hg, mg, lg = codes[pl.ds(r, 16), :], whi[pl.ds(r, 16), :], wmid[pl.ds(r, 16), :], wlo[pl.ds(r, 16), :]
        bc = [[jnp.broadcast_to(x[:, k:k + 1], (16, 128)) for k in range(DEG)] for x in (cg, hg, mg, lg)]
        for t in range(TILES):
            io = iocode[t]
            accs = [jnp.zeros((16, 128), BF16) for _ in range(PIECES)]
            for k in range(DEG):
                eq = bc[0][k] == io
                accs = [jnp.where(eq, bc[1 + p][k], accs[p]) for p in range(PIECES)]
            for p in range(PIECES):
                a3[pl.ds(pl.multiple_of(base + p * BM, 16), 16), t * 128:(t + 1) * 128] = accs[p]
        return carry

    lax.fori_loop(0, ROWS // 16, build, 0)

    for c in first:
        c.wait()

    def layer_one(i, carry):
        a = pl.multiple_of(i * BM * PIECES, BM)
        r = pl.multiple_of(i * BM, BM)
        acc = jnp.dot(a3[pl.ds(a, BM * PIECES), :], e1[...], preferred_element_type=F32)
        z = (acc[0:BM] + (acc[BM:2 * BM] + acc[2 * BM:])).astype(BF16)
        z1[pl.ds(r, BM), :] = z
        h = jnp.dot(z, w1b[...], preferred_element_type=F32)
        e2[pl.ds(r, BM), :] = jnp.maximum(h, 0.0).astype(BF16)
        return carry

    lax.fori_loop(0, NB, layer_one, 0)

    for b in range(4):
        send2[b * 256:(b + 1) * 256, :] = jnp.dot(
            sel[b * 256:(b + 1) * 256, :], e2[0:ROWS, :], preferred_element_type=F32).astype(BF16)
    second = []
    for d in range(1, DEVS):
        src = pl.multiple_of(peer(d) * HALO, HALO)
        second.append(remote(2, d, send2.at[pl.ds(src, HALO), :], e2.at[pl.ds(own, HALO), :]))
    for c in second:
        c.start()
    for c in second:
        c.wait()

    def layer_two(i, carry):
        a = pl.multiple_of(i * BM * PIECES, BM)
        r = pl.multiple_of(i * BM, BM)
        acc = jnp.dot(a3[pl.ds(a, BM * PIECES), :], e2[...], preferred_element_type=F32)
        z2[pl.ds(r, BM), :] = (acc[0:BM] + (acc[BM:2 * BM] + acc[2 * BM:])).astype(BF16)
        return carry

    lax.fori_loop(0, NB, layer_two, 0)

    nt = (((1,), (1,)), ((), ()))
    logits = lax.dot_general(w2t, z2[...], nt, preferred_element_type=F32)
    sub = lax.broadcasted_iota(jnp.int32, (8, ROWS), 0)
    logits = jnp.where(sub < CLS, logits, -BIG)
    shifted = logits - jnp.max(logits, axis=0, keepdims=True)
    expd = jnp.where(sub < CLS, jnp.exp(shifted), 0.0)
    log_prob = shifted - jnp.log(jnp.sum(expd, axis=0, keepdims=True))
    onehot = labels[...] == sub
    total = jnp.sum(cnts[...], axis=0)[0:1, 0:1]
    picked = jnp.sum(jnp.where(onehot, log_prob, 0.0), axis=0, keepdims=True)
    loss_part = jnp.sum(picked * maskf, axis=1, keepdims=True)
    prob = jnp.where(sub < CLS, jnp.exp(log_prob), 0.0)
    g2t = ((prob - onehot.astype(F32)) * (maskf / total)).astype(BF16)

    g2sum = jnp.dot(g2t, z2[...], preferred_element_type=F32)
    srow = lax.broadcasted_iota(jnp.int32, (8, HID), 0)
    small[...] = jnp.where(srow == CLS, loss_part, g2sum)
    smallr[me] = small[...]

    ut[...] = jnp.zeros(ut.shape, F32)
    for i in range(NB):
        g = g2t[:, i * BM:(i + 1) * BM]
        lhs = jnp.concatenate([g, g, g], axis=1)
        ut[...] += jnp.dot(lhs, a3[i * BM * PIECES:(i + 1) * BM * PIECES, :], preferred_element_type=F32)
    for q in range(DEVS):
        sendu[q, :, 0:HALO] = ut[:, ROWS + q * HALO:ROWS + (q + 1) * HALO]
    third = []
    for d in range(1, DEVS):
        third.append(remote(3, d, sendu.at[peer(d)], recvu.at[me]))
        third.append(remote(4, d, small, smallr.at[me]))
    recvu[me] = jnp.zeros((8, 128), F32)
    for c in third:
        c.start()
    for c in third:
        c.wait()

    for q in range(DEVS):
        rt[:, q * HALO:(q + 1) * HALO] = recvu[q, :, 0:HALO]
    pieces = jnp.concatenate([x.astype(F32) for x in split3(rt[...])], axis=0).astype(BF16)
    back = jnp.dot(pieces, sel[...], preferred_element_type=F32)
    u = ut[:, 0:ROWS] + (back[0:8] + (back[8:16] + back[16:24]))
    upieces = jnp.concatenate([x.astype(F32) for x in split3(u)], axis=0).astype(BF16)
    w2f = w2t.astype(F32)
    w2x = jnp.concatenate([w2f, w2f, w2f], axis=0).astype(BF16)
    tn = (((0,), (0,)), ((), ()))
    d_h1 = lax.dot_general(upieces, w2x, tn, preferred_element_type=F32)
    g1 = jnp.where(e2[0:ROWS, :].astype(F32) > 0, d_h1, 0.0).astype(BF16)
    part[...] = lax.dot_general(z1[...], g1, tn, preferred_element_type=F32)

    rows = FPAD // DEVS
    fourth = []
    for d in range(1, DEVS):
        src = pl.multiple_of(peer(d) * rows, rows)
        fourth.append(remote(5, d, part.at[pl.ds(src, rows), :], rsr.at[me]))
    for c in fourth:
        c.start()
    mine = pl.multiple_of(me * rows, rows)
    rsr[me] = part[pl.ds(mine, rows), :]
    for c in fourth:
        c.wait()
    red[...] = jnp.sum(rsr[...], axis=0)
    fifth = []
    for d in range(1, DEVS):
        fifth.append(remote(6, d, red, agb.at[pl.ds(mine, rows), :]))
    for c in fifth:
        c.start()
    agb[pl.ds(mine, rows), :] = red[...]
    tot = jnp.sum(smallr[...], axis=0)
    loss_o[...] = -tot[CLS:CLS + 1, 0:1] / total
    w2s[:, 0:8] = tot.T
    g2_o[...] = w2s[:, 0:CLS]
    for c in fifth:
        c.wait()
    g1_o[...] = agb[0:FIN, :]


def solution(mesh):
    def device_step(feats, w_one, w_two, send_idx, send_count, edge_src, edge_wt, labels, label_mask):
        vm = pl.BlockSpec(memory_space=pltpu.VMEM)
        loss, g1, g2 = pl.pallas_call(
            kernel,
            out_shape=(jax.ShapeDtypeStruct((1, 1), F32), jax.ShapeDtypeStruct((FIN, HID), F32),
                       jax.ShapeDtypeStruct((HID, CLS), F32)),
            in_specs=[vm] * 9,
            out_specs=(vm, vm, vm),
            scratch_shapes=[
                pltpu.VMEM((NB * BM * PIECES, EXT), BF16),
                pltpu.VMEM((EXT, FPAD), BF16),
                pltpu.VMEM((ROWS, FPAD), BF16),
                pltpu.VMEM((EXT, HID), BF16),
                pltpu.VMEM((ROWS, HID), BF16),
                pltpu.VMEM((DEVS * HALO, ROWS), BF16),
                pltpu.VMEM((DEVS * HALO, FPAD), BF16),
                pltpu.VMEM((DEVS * HALO, HID), BF16),
                pltpu.VMEM((128, 128), jnp.int32),
                pltpu.VMEM((128, 128), F32),
                pltpu.VMEM((ROWS, 128), BF16),
                pltpu.VMEM((ROWS, 128), BF16),
                pltpu.VMEM((ROWS, 128), BF16),
                pltpu.VMEM((ROWS, 128), BF16),
                pltpu.VMEM((TILES, 16, 128), BF16),
                pltpu.VMEM((128, 128), jnp.int32),
                pltpu.VMEM((FPAD, HID), BF16),
                pltpu.VMEM((HID, 128), F32),
                pltpu.VMEM((DEVS, 8, 128), F32),
                pltpu.VMEM((8, 128), F32),
                pltpu.VMEM((DEVS, 8, 128), F32),
                pltpu.VMEM((DEVS, 8, 128), F32),
                pltpu.VMEM((8, HID), F32),
                pltpu.VMEM((DEVS, 8, HID), F32),
                pltpu.VMEM((8, DEVS * HALO), F32),
                pltpu.VMEM((FPAD, HID), F32),
                pltpu.VMEM((DEVS, FPAD // DEVS, HID), F32),
                pltpu.VMEM((FPAD // DEVS, HID), F32),
                pltpu.VMEM((FPAD, HID), F32),
                pltpu.VMEM((8, EXT), F32),
                pltpu.SemaphoreType.DMA((7, DEVS)),
                pltpu.SemaphoreType.DMA((7, DEVS)),
            ],
            compiler_params=pltpu.CompilerParams(
                collective_id=0, has_side_effects=True, vmem_limit_bytes=67043328),
            name="gcn_step",
        )(feats, w_one, w_two, send_idx, send_count.reshape(1, DEVS), edge_src, edge_wt,
          labels.reshape(1, ROWS), label_mask.reshape(1, ROWS))
        return loss.reshape(()), g1, g2

    row, vec = P("graph", None), P("graph")
    return jax.shard_map(device_step, mesh=mesh, in_specs=(row, P(), P(), row, vec, row, row, vec, vec),
                         out_specs=(P(), P(), P()), check_vma=False)
```

time: 692 us -> 214 us (0.31)
  local copies, waits for them, and re-layouts: 326 us -> 12 us
  other arithmetic: 201 us -> 0 us
  Pallas kernels: 0 us -> 199 us
  blocking collectives: 65.9 us -> 0 us
  waiting for transfers between devices: 59.8 us -> 0 us
  between operations: 16.8 us -> 2.33 us
  starting transfers between devices: 11 us -> 0 us
  matrix products: 7.77 us -> 0 us
    gather x4 -> x0, local copies, waits for them, and re-layouts: 203 us -> none  [the longest x2 195 us: aggregate(): ext_rows[edge_src].astype(jnp.float32) * edge_wt[:, :, None]]
    pallas_call x0 -> x1, Pallas kernels: none -> 199 us  [device_step(): pl.pallas_call(kernel, out_shape=(jax.ShapeDtypeStruct((1, 1), F32), jax....]
    scatter-add x2 -> x0, other arithmetic: 152 us -> none  [the longest x1 145 us: device_step(): jax.ops.segment_sum(contrib, flat_src, num_segments=row_count + dev_count...]
    convert_element_type x2 -> x0, local copies, waits for them, and re-layouts: 68.5 us -> none  [aggregate(): ext_rows[edge_src].astype(jnp.float32) * edge_wt[:, :, None]]
    psum x2 -> x0, blocking collectives: 65.9 us -> none  [the longest x1 34 us: device_step(): label_total = lax.psum(jnp.sum(mask_f), 'graph')]
    mul x3 -> x0, local copies, waits for them, and re-layouts: 41.9 us -> none  [the longest x2 41.1 us: device_step(): edge_wt[:, :, None] * d_z2[:, None, :]]
    reduce_sum x5 -> x0, other arithmetic: 40.8 us -> none  [the longest x2 39.5 us: aggregate(): jnp.sum(ext_rows[edge_src].astype(jnp.float32) * edge_wt[:, :, None], axi...]
    psum x1 -> x0, waiting for transfers between devices: 30.5 us -> none  [device_step(): lax.psum(jnp.einsum('nf,nh->fh', z_one, d_y1, preferred_element_type=jnp....]
  transfers between devices with their start and end apart: 4 -> 0, of which waited for: 3 -> 0; matrix products, arithmetic and copies ran while one was open for 1% -> 0% of each run, Pallas kernels for 0% -> 0%
where the time goes in v1:
time: 214 us
  Pallas kernels  199 us (93%)
  local copies, waits for them, and re-layouts  12 us (6%)
  between operations  2.33 us (1%)
    pallas_call x1, Pallas kernels, device_step(): pl.pallas_call(kernel, out_shape=(jax.ShapeDtypeStruct((1, 1), F32), jax....  199 us
    unnamed x8, local copies, waits for them, and re-layouts  12 us

profile of v1, /device:TPU:0, one launch (start us, length us, event | category | flops | bytes accessed | tf_op | source)
XLA Modules:
  0.0 213.8 jit_solution(13957649809557469949)
XLA Ops:
  0.6 0.0 copy-start
  0.6 1.6 copy.13.w2
  2.3 2.3 %copy.14.esrc = s32[2048,12]{1,0:T(8,128)} copy(s32[2048,12]{0,1:T(8,128)} %param.14) | data formatting | bytes 196608 | tf_op args[5]
  4.5 2.2 %copy.15.ewt = f32[2048,12]{1,0:T(8,128)} copy(f32[2048,12]{0,1:T(8,128)} %param.15) | data formatting | bytes 196608 | tf_op args[6]
  6.8 0.0 copy-done
  6.8 2.4 %copy.12.feats = bf16[2048,500]{1,0:T(8,128)(2,1)} copy(bf16[2048,500]{0,1:T(8,128)(2,1)S(1)} %copy-done) | data formatting | bytes 4096000 | tf_op args[0]
  9.2 199.4 %gcn_step.1 = (f32[1,1]{1,0:T(1,128)}, f32[500,256]{1,0:T(8,128)}, f32[256,7]{1,0:T(8,128)}) custom-call(bf16[2048,500]{1,0:T(8,128)(2,1)} %copy.12.feats, f32[500,256]{1,0:T(8,128)} %w1.1, f32[256,7]{1,0:T(8,128)} %copy.13.w2, s32[16,64]{1,0:T(8,128)} %sidx.1, s32[1,16]{1,0:T(1,128)} %bitcast.6, s32[2048,12]{1,0:T(8,128)} %copy.14.esrc, ...), custom_call_target="tpu_custom_call" | custom-call | tf_op jit(solution)/shard_map/gcn_step/pallas_call | solution.py:258
  208.6 1.6 copy.16
  210.8 1.9 copy.20
Async XLA Ops:
  0.6 6.1 %copy-start = (bf16[2048,500]{0,1:T(8,128)(2,1)S(1)}, bf16[2048,500]{0,1:T(8,128)(2,1)}, u32[]{:S(2)}) copy-start(bf16[2048,500]{0,1:T(8,128)(2,1)} %param.9) | copy-start | bytes 6144004
